TPU v7x, 32 devices: a whole 2x2x4 slice. The times are simulated.
32 devices in a mesh: dp: 4 (over x, core), vocab: 8 (over z, y).
Axes of the slice: x: 2, y: 2, z: 4, core: 2. Of those that a mesh axis runs over, the one named last changes fastest.
Arguments:
- hidden: bfloat16 [128, 8192], P(('dp', 'vocab')), may hold values from -350 to 350
- lm_head: bfloat16 [8192, 128256], P(None, ('dp', 'vocab')), may hold values from -0.0625 to 0.0625
- targets: int32 [128], P(('dp', 'vocab')), may hold values from 0 to 128255
- segment: int32 [128], P(('dp', 'vocab')), may hold values from 0 to 32, as said below
- pad_mask: int32 [128], P(('dp', 'vocab')), may hold values from 0 to 1, as said below
- seq_bench: int32 [33], replicated, may hold values from 0 to 7
Outputs:
- token_nll: float32 [128], P(('dp', 'vocab'))
- bench_total: float32 [8], replicated
- bench_count: float32 [8], replicated
Inputs may be any that keep to these rules, and one draw needn't show every extreme that they name: `segment`: sequence numbers never fall along the pack; each aligned block of 4 tokens holds exactly one place inside it where the number rises by one, and the number does not change between one block's last token and the next block's first. `pad_mask`: the last token of each aligned block of 4 tokens is real.
All inputs are finite; a program needn't handle non-finite values.
Results may differ from a plain program's by a relative error of at most 0.0003.
Values may be sent and summed in bfloat16 or wider, within the bound.
A program may use at most 128 MiB of HBM per device.

v0:
```python
import functools
import math

import jax
import jax.numpy as jnp
from jax import lax
from jax.experimental import pallas as pl
from jax.experimental.pallas import tpu as pltpu
from jax.sharding import PartitionSpec as P

NBENCH = 8
MESH = pl.DeviceIdType.MESH


def kernel(dims, hid, meta, w_hbm, out, part, g, wbuf, acc, mbuf, mine, sbuf,
           wsem, rsem, psem, fsem, msem, qsem, ssem, s1sem, s2sem):
    X, Y, Z, V, N, kc, nk, nbuf, tok_dev = dims
    dp, v = lax.axis_index("dp"), lax.axis_index("vocab")
    me = dp * V + v
    x, core = dp // 2, lax.rem(dp, 2)
    z, y = v // Y, lax.rem(v, Y)
    rows2 = 2 * tok_dev
    tokens = N * tok_dev
    half, quarter = nk // 2, nk // 4

    def dev(xx, yy, zz, cc):
        return (xx * 2 + cc, zz * Y + yy)

    def slot_of(xx, yy, zz):
        return (yy * X + xx) * Z + zz

    def chunk(i):
        return lax.rem(core * half + i, nk)

    def wcopy(k, s):
        return pltpu.make_async_copy(
            w_hbm.at[:, pl.ds(pl.multiple_of(chunk(k) * kc, kc), kc)], wbuf.at[s], wsem.at[s])

    for k in range(nbuf):
        wcopy(k, k).start()
    acc[...] = jnp.zeros_like(acc)

    barrier = pltpu.get_barrier_semaphore()

    def greet(d, c):
        t = lax.rem(me + d, N)
        pl.semaphore_signal(barrier, inc=1, device_id=(t // V, lax.rem(t, V)), device_id_type=MESH)
        return c

    lax.fori_loop(1, N, greet, 0)
    pl.semaphore_wait(barrier, N - 1)

    partner = (x * 2 + 1 - core, v)
    first = pltpu.make_async_remote_copy(hid, part, fsem.at[0], fsem.at[1],
                                         device_id=partner, device_id_type=MESH)
    first.start()
    first.wait_recv()
    own = hid[...].astype(jnp.float32)
    other = part[...].astype(jnp.float32)
    both = jnp.where(core == 0, jnp.concatenate([own, other], 0),
                     jnp.concatenate([other, own], 0)).astype(jnp.bfloat16)
    my_slot = slot_of(x, y, z)
    for k in range(nk):
        g[k, pl.ds(pl.multiple_of(my_slot * rows2, rows2), rows2), :] = both[:, k * kc:(k + 1) * kc]

    def mcopy(t, src_dev):
        return pltpu.make_async_remote_copy(
            meta, mbuf.at[src_dev], s1sem.at[t], msem.at[src_dev],
            device_id=(t // V, lax.rem(t, V)), device_id_type=MESH)

    def msend(d, c):
        mcopy(lax.rem(me + d, N), me).start()
        return c

    lax.fori_loop(1, N, msend, 0)
    mbuf[me] = meta[...]

    sends = []

    def piece(s, start, count):
        return g.at[pl.ds(start, count), pl.ds(pl.multiple_of(s * rows2, rows2), rows2), :]

    def send(s, start, count, sem, to):
        ref = piece(s, start, count)
        copy = pltpu.make_async_remote_copy(ref, ref, ssem.at[len(sends)], sem,
                                            device_id=to, device_id_type=MESH)
        copy.start()
        sends.append(copy)

    def arrived(s, start, count, sem):
        ref = piece(s, start, count)
        pltpu.make_async_copy(ref, ref, sem).wait()

    k0 = core * half
    kp = (1 - core) * half
    back = lambda a, d, n: lax.rem(a + n - d, n)
    fwd = lambda a, d, n: lax.rem(a + d, n)

    def plane(s):
        for dx in range(1, X):
            send(s, k0, half, rsem.at[s, 0], dev(fwd(x, dx, X), y, z, core))
        for dy in range(1, Y):
            send(s, k0, half, rsem.at[s, 0], dev(x, fwd(y, dy, Y), z, core))

    for dz in range(1, Z):
        send(my_slot, k0, half, rsem.at[my_slot, 0], dev(x, y, fwd(z, dz, Z), core))
    plane(my_slot)

    def forward(dz):
        zz = back(z, dz, Z)
        for dx in range(1, X):
            s = slot_of(back(x, dx, X), y, zz)
            arrived(s, k0, half, rsem.at[s, 0])
            for dy in range(1, Y):
                send(s, k0, quarter, rsem.at[s, 0], dev(x, fwd(y, dy, Y), z, core))
            send(s, k0, half, psem.at[s], partner)
        for dy in range(1, Y):
            s = slot_of(x, back(y, dy, Y), zz)
            arrived(s, k0, half, rsem.at[s, 0])
            for dx in range(1, X):
                send(s, k0 + quarter, quarter, rsem.at[s, 1], dev(fwd(x, dx, X), y, z, core))
            send(s, k0, half, psem.at[s], partner)

    for dz in range(1, Z):
        s = slot_of(x, y, back(z, dz, Z))
        arrived(s, k0, half, rsem.at[s, 0])
        plane(s)
        send(s, k0, half, psem.at[s], partner)
        forward(dz - 1)
    forward(Z - 1)
    for dz in range(Z):
        for dx in range(1, X):
            for dy in range(1, Y):
                s = slot_of(back(x, dx, X), back(y, dy, Y), back(z, dz, Z))
                arrived(s, k0, quarter, rsem.at[s, 0])
                arrived(s, k0 + quarter, quarter, rsem.at[s, 1])
                send(s, k0, half, psem.at[s], partner)
    def step(k, c):
        s = lax.rem(k, nbuf)
        wcopy(k, s).wait()
        acc[...] += lax.dot_general(wbuf[s], g[chunk(k)], (((1,), (1,)), ((), ())),
                                    preferred_element_type=jnp.float32)

        @pl.when(k + nbuf < nk)
        def _():
            wcopy(k + nbuf, s).start()

        return c

    lax.fori_loop(0, half, step, 0)
    for dz in range(Z):
        for dx in range(X):
            for dy in range(Y):
                if dz or dx or dy:
                    s = slot_of(back(x, dx, X), back(y, dy, Y), back(z, dz, Z))
                    arrived(s, kp, half, psem.at[s])
    lax.fori_loop(half, nk, step, 0)

    def mrecv(d, c):
        t = lax.rem(me + d, N)
        mcopy(t, t).wait()
        return c

    lax.fori_loop(1, N, mrecv, 0)
    info = jnp.sum(mbuf[...], axis=0)
    voc_dev = acc.shape[0]
    wanted = info[:1].astype(jnp.int32) - me * voc_dev
    logits = acc[...]
    top = jnp.max(logits, axis=0, keepdims=True)
    expsum = jnp.sum(jnp.exp(logits - top), axis=0, keepdims=True)
    entry = lax.broadcasted_iota(jnp.int32, logits.shape, 0)
    picked = jnp.sum(jnp.where(entry == wanted, logits, 0.0), axis=0, keepdims=True)
    mine[...] = jnp.concatenate([top + jnp.log(expsum), picked], axis=0)

    def qcopy(t, src_dev):
        return pltpu.make_async_remote_copy(
            mine, sbuf.at[src_dev], s2sem.at[t], qsem.at[src_dev],
            device_id=(t // V, lax.rem(t, V)), device_id_type=MESH)

    def qsend(d, c):
        qcopy(lax.rem(me + d, N), me).start()
        return c

    def qrecv(d, c):
        t = lax.rem(me + d, N)
        qcopy(t, t).wait()
        return c

    lax.fori_loop(1, N, qsend, 0)
    sbuf[me] = mine[...]
    first.wait_send()
    for copy in sends:
        copy.wait_send()
    lax.fori_loop(1, N, qrecv, 0)

    allstat = sbuf[...]
    lse = allstat[:, 0, :]
    top = jnp.max(lse, axis=0, keepdims=True)
    total = top + jnp.log(jnp.sum(jnp.exp(lse - top), axis=0, keepdims=True))
    nll = total - jnp.sum(allstat[:, 1, :], axis=0, keepdims=True)
    kind = info[1:2]
    row = lax.broadcasted_iota(jnp.int32, (NBENCH, tokens), 0)
    lane = lax.broadcasted_iota(jnp.int32, (NBENCH, tokens), 1)
    hot = kind == row.astype(jnp.float32)
    at = my_slot * rows2 + core * tok_dev
    own_nll = jnp.sum(jnp.where(lane == at + row, nll, 0.0), axis=1, keepdims=True)
    bench_total = jnp.sum(jnp.where(hot, nll, 0.0), axis=1, keepdims=True)
    bench_count = jnp.sum(jnp.where(hot, 1.0, 0.0), axis=1, keepdims=True)
    place = lax.broadcasted_iota(jnp.int32, (NBENCH, 128), 1)
    out[...] = jnp.where(place == 0, own_nll, jnp.where(place == 1, bench_total, bench_count))


def solution(mesh):
    ndp, V = mesh.shape["dp"], mesh.shape["vocab"]
    N = ndp * V
    X = max(1, ndp // 2)
    Y = math.gcd(X, V)
    Z = V // Y

    def body(hidden, lm_head, targets, segment, pad_mask, seq_bench):
        tok_dev, depth = hidden.shape
        voc_dev = lm_head.shape[1]
        tokens = N * tok_dev
        dp, v = lax.axis_index("dp"), lax.axis_index("vocab")
        slot = (lax.rem(v, Y) * X + dp // 2) * Z + v // Y
        start = slot * 2 * tok_dev + lax.rem(dp, 2) * tok_dev
        last = (dp * V + v == N - 1)
        same = jnp.concatenate([segment[1:] == segment[:-1], jnp.logical_not(last)[None]])
        keep = (pad_mask != 0) & same
        hot = segment[:, None] == lax.broadcasted_iota(jnp.int32, (1, seq_bench.shape[0]), 1)
        bench = jnp.sum(jnp.where(hot, seq_bench[None, :], 0), axis=1)
        kind = jnp.where(keep, bench, NBENCH)
        lane = lax.broadcasted_iota(jnp.int32, (2, tokens), 1) - start
        both = jnp.stack([targets, kind]).astype(jnp.float32)
        meta = jnp.zeros((2, tokens), jnp.float32)
        for j in range(tok_dev):
            meta = jnp.where(lane == j, both[:, j:j + 1], meta)

        nk = 16
        kc = depth // nk
        wbytes = kc * (-(-voc_dev // 8) * 8) * 2
        held = tokens * depth * 2 + tokens * (-(-voc_dev // 128) * 128) * 4
        nbuf = max(2, min(nk, ((61 << 20) - held) // wbytes))
        nsend = (Z - 1) + Z * (X + Y - 2) + 2 * Z * (X - 1) * (Y - 1) + Z * X * Y - 1
        dims = (X, Y, Z, V, N, kc, nk, nbuf, tok_dev)
        vmem = pl.BlockSpec(memory_space=pltpu.VMEM)
        dma = pltpu.SemaphoreType.DMA
        res = pl.pallas_call(
            functools.partial(kernel, dims),
            out_shape=jax.ShapeDtypeStruct((NBENCH, 128), jnp.float32),
            in_specs=[vmem, vmem, pl.BlockSpec(memory_space=pltpu.MemorySpace.HBM)],
            out_specs=vmem,
            scratch_shapes=[
                pltpu.VMEM((tok_dev, depth), jnp.bfloat16),
                pltpu.VMEM((nk, tokens, kc), jnp.bfloat16),
                pltpu.VMEM((nbuf, voc_dev, kc), jnp.bfloat16),
                pltpu.VMEM((voc_dev, tokens), jnp.float32),
                pltpu.VMEM((N, 2, tokens), jnp.float32),
                pltpu.VMEM((2, tokens), jnp.float32),
                pltpu.VMEM((N, 2, tokens), jnp.float32),
                dma((nbuf,)),
                dma((Z * X * Y, 2)),
                dma((Z * X * Y,)),
                dma((2,)),
                dma((N,)),
                dma((N,)),
                dma((nsend,)),
                dma((N,)),
                dma((N,)),
            ],
            compiler_params=pltpu.CompilerParams(
                collective_id=0, has_side_effects=True, vmem_limit_bytes=67043328),
        )(hidden, meta, lm_head.T)
        return res[:tok_dev, 0], res[:, 1], res[:, 2]

    both = ("dp", "vocab")
    in_specs = (P(both, None), P(None, both), P(both), P(both), P(both), P())
    return jax.shard_map(body, mesh=mesh, in_specs=in_specs, out_specs=(P(both), P(), P()),
                         check_vma=False)
```

profile of v0, /device:TPU:0, one launch (start us, length us, event | category | flops | bytes accessed | tf_op | source)
XLA Modules:
  0.0 62.8 jit_solution(17151332796306867031)
XLA Ops:
  0.7 0.9 %select_reduce_fusion = s32[4]{0:T(128)S(1)} fusion(s32[33]{0:T(128)} %param.11, s32[4]{0:T(128)} %param.9), kind=kLoop, calls=%fused_computation.3 | loop fusion | flops 392 | bytes 164 | tf_op jit(solution)/shard_map/reduce_sum | solution.py:231
  1.6 0.8 %slice_compare_fusion = pred[3]{0:T(512)(128)(4,1)S(1)} fusion(s32[4]{0:T(128)} %param.9), kind=kLoop, calls=%fused_computation.13 | loop fusion | flops 3 | bytes 27 | tf_op jit(solution)/shard_map/eq | solution.py:228
  2.4 0.7 %fusion.5 = s32[1,4]{1,0:T(1,128)S(1)} fusion(s32[4]{0:T(128)S(1)} %select_reduce_fusion, pred[1]{0:T(512)(128)(4,1)} %bitcast.1, pred[3]{0:T(512)(128)(4,1)S(1)} %slice_compare_fusion, s32[4]{0:T(128)} %param.10), kind=kLoop, calls=%fused_computation.19 | loop fusion | flops 16 | bytes 52 | tf_op jit(solution)/shard_map/stack | solution.py:234
  3.1 0.7 %add_convert_fusion = f32[2,4]{1,0:T(2,128)S(1)} fusion(s32[1,4]{1,0:T(1,128)S(1)} %fusion.5, s32[1,4]{1,0:T(1,128)} %bitcast.6), kind=kLoop, calls=%fused_computation.7 | loop fusion | flops 16 | bytes 64 | tf_op jit(solution)/shard_map/convert_element_type | solution.py:234
  3.8 0.2 slice_reduce_fusion.3
  4.0 0.7 %select_select_fusion.meta = f32[2,128]{1,0:T(2,128)} fusion(pred[128]{0:T(512)(128)(4,1)S(1)} %get-tuple-element.9, pred[128]{0:T(512)(128)(4,1)S(1)} %get-tuple-element.10, pred[128]{0:T(512)(128)(4,1)S(1)} %get-tuple-element.11, pred[128]{0:T(512)(128)(4,1)S(1)} %get-tuple-element.12, f32[2]{0:T(128)S(1)} %get-tuple-element.6, f32[2]{0:T(128)S(1)} %get-tuple-element.7, ...), kind=kLoop, calls=%fused_computation.8 | loop fusion | flops 1024 | bytes 1568 | tf_op jit(solution)/shard_map/jit(_where)/select_n | solution.py:237
  4.6 55.4 %shard_map.85 = f32[8,128]{1,0:T(8,128)} custom-call(bf16[4,8192]{1,0:T(4,128)(2,1)} %hid.1, f32[2,128]{1,0:T(2,128)} %select_select_fusion.meta, bf16[4008,8192]{1,0:T(8,128)(2,1)} %bitcast.5), custom_call_target="tpu_custom_call" | custom-call | tf_op jit(solution)/shard_map/pallas_call | solution.py:248
  60.0 1.5 %slice_reduce_fusion = (f32[8]{0:T(128)}, f32[8]{0:T(128)}) fusion(f32[8,128]{1,0:T(8,128)} %shard_map.85), kind=kLoop, calls=%fused_computation | loop fusion | bytes 128 | tf_op jit(solution)/shard_map/slice | solution.py:274
  61.5 1.3 %slice_reduce_fusion.2 = f32[4]{0:T(128)} fusion(f32[8,128]{1,0:T(8,128)} %shard_map.85), kind=kLoop, calls=%fused_computation.2 | loop fusion | bytes 32 | tf_op jit(solution)/shard_map/slice | solution.py:274
  (2 shorter events, 0.0 us)
where the time goes:
time: 63.1 us; the launch traced here: 62.8 us
  Pallas kernels  55.4 us (88%)
  other arithmetic  3.73 us (6%)
  local copies, waits for them, and re-layouts  3.01 us (5%)
  between operations  0.7 us (1%)
    pallas_call x1, Pallas kernels, body(): pl.pallas_call(functools.partial(kernel, dims), out_shape=jax.ShapeDtypeS...  55.4 us
    slice x2, local copies, waits for them, and re-layouts, body(): return (res[:tok_dev, 0], res[:, 1], res[:, 2])  2.8 us

commit v1 on v0

v1 whole, which is shorter than its diff:
```python
import functools
import math

import jax
import jax.numpy as jnp
from jax import lax
from jax.experimental import pallas as pl
from jax.experimental.pallas import tpu as pltpu
from jax.sharding import PartitionSpec as P

NBENCH = 8
MESH = pl.DeviceIdType.MESH


def kernel(dims, hid, tgt, seg, pad, kinds, w_hbm, nll_out, total_out, count_out,
           g, wbuf, acc, meta, tgt_v, seg_v, pad_v, kinds_v, mine, sbuf,
           wsem, hsem, isem, zrecv, precv, crecv, zsend, psend, csend,
           mzrecv, mprecv, mcrecv, mzsend, mpsend, mcsend, qsend, qrecv):
    X, Y, Z, V, N, kc, nk, nbuf, td, lead_z, lead_p = dims
    XY, S = X * Y, X * Y * Z
    dp, v = lax.axis_index("dp"), lax.axis_index("vocab")
    me = dp * V + v
    x, core = dp // 2, lax.rem(dp, 2)
    z, y = v // Y, lax.rem(v, Y)
    xy = x * Y + y
    tokens = N * td
    at = (core * S + xy * Z + z) * td

    def zpeer(d):
        zz = lax.rem(z + d, Z)
        return (dp, zz * Y + y), zz

    def ppeer(d):
        t = lax.rem(xy + d, XY)
        return ((t // Y) * 2 + core, z * Y + lax.rem(t, Y)), t

    partner = (x * 2 + 1 - core, v)
    peers = [zpeer(d)[0] for d in range(1, Z)] + [ppeer(d)[0] for d in range(1, XY)] + [partner]

    own = pltpu.make_async_copy(hid, g.at[pl.ds(pl.multiple_of(at, td), td), :], hsem)
    own.start()
    loads = [pltpu.make_async_copy(a, b, isem.at[i]) for i, (a, b) in enumerate(
        ((tgt, tgt_v), (seg, seg_v), (pad, pad_v), (kinds, kinds_v)))]
    for copy in loads:
        copy.start()

    def wcopy(k):
        s = lax.rem(k, nbuf)
        return pltpu.make_async_copy(
            w_hbm.at[:, pl.ds(pl.multiple_of(k * kc, kc), kc)], wbuf.at[s], wsem.at[s])

    for k in range(nbuf):
        wcopy(k).start(priority=1)

    barrier = pltpu.get_barrier_semaphore()
    for peer in peers:
        pl.semaphore_signal(barrier, inc=1, device_id=peer, device_id_type=MESH)

    for copy in loads:
        copy.wait()
    nseq = kinds_v.shape[1]
    last = me == N - 1
    lane = lax.broadcasted_iota(jnp.int32, (1, tokens), 1) - at
    seqs = lax.broadcasted_iota(jnp.int32, (1, nseq), 1)
    wanted = jnp.zeros((1, tokens), jnp.int32)
    kind = jnp.zeros((1, tokens), jnp.int32)
    for j in range(td):
        s = seg_v[:, j:j + 1]
        bench = jnp.sum(jnp.where(seqs == s, kinds_v[...], 0), axis=1, keepdims=True)
        same = s == seg_v[:, j + 1:j + 2] if j + 1 < td else jnp.broadcast_to(jnp.logical_not(last), (1, 1))
        keep = same & (pad_v[:, j:j + 1] != 0)
        wanted = jnp.where(lane == j, tgt_v[:, j:j + 1], wanted)
        kind = jnp.where(lane == j, jnp.where(keep, bench, NBENCH), kind)
    meta[core * S + xy * Z + z] = jnp.concatenate([wanted, kind], axis=0)
    own.wait()
    pl.semaphore_wait(barrier, len(peers))

    def cols(p):
        return pl.ds(pl.multiple_of(p * kc, kc), kc)

    def rows(first, count):
        return pl.ds(pl.multiple_of((core * S + first) * td, td), count * td)

    def remote(src, send, recv, to):
        return pltpu.make_async_remote_copy(src, src, send, recv, device_id=to, device_id_type=MESH)

    def zcopy(p, d):
        ref = g.at[rows(xy * Z + z, 1), cols(p)]
        return remote(ref, zsend.at[p, d], zrecv.at[p, z], zpeer(d)[0])

    def pcopy(p, d):
        ref = g.at[rows(xy * Z, Z), cols(p)]
        return remote(ref, psend.at[p, d], precv.at[p, xy], ppeer(d)[0])

    def ccopy(p):
        ref = g.at[rows(0, S), cols(p)]
        return remote(ref, csend.at[p], crecv.at[p], partner)

    def arrived(ref, sem):
        pltpu.make_async_copy(ref, ref, sem).wait()

    def send_z(p, c):
        for d in range(1, Z):
            zcopy(p, d).start()
        return c

    def from_z(p, c=0):
        for d in range(1, Z):
            zz = zpeer(d)[1]
            arrived(g.at[rows(xy * Z + zz, 1), cols(p)], zrecv.at[p, zz])
        for d in range(1, XY):
            pcopy(p, d).start()
        return c

    def from_p(p, c=0):
        for d in range(1, XY):
            t = ppeer(d)[1]
            arrived(g.at[rows(t * Z, Z), cols(p)], precv.at[p, t])
        ccopy(p).start()
        return c

    lax.fori_loop(0, nk, send_z, 0)

    def mref(first, count):
        return meta.at[pl.ds(core * S + first, count)]

    mz = [remote(mref(xy * Z + z, 1), mzsend.at[d], mzrecv.at[z], zpeer(d)[0]) for d in range(1, Z)]
    mp = [remote(mref(xy * Z, Z), mpsend.at[d], mprecv.at[xy], ppeer(d)[0]) for d in range(1, XY)]
    mc = remote(mref(0, S), mcsend.at[0], mcrecv.at[0], partner)
    for copy in mz:
        copy.start()
    acc[...] = jnp.zeros_like(acc)

    for p in range(lead_z):
        from_z(p)
    for d in range(1, Z):
        zz = zpeer(d)[1]
        arrived(mref(xy * Z + zz, 1), mzrecv.at[zz])
    for copy in mp:
        copy.start()
    for p in range(lead_p):
        from_p(p)

    def step(k, c):
        @pl.when(k + lead_z < nk)
        def _():
            from_z(k + lead_z)

        @pl.when(k + lead_p < nk)
        def _():
            from_p(k + lead_p)

        arrived(g.at[pl.ds(pl.multiple_of((1 - core) * S * td, S * td), S * td), cols(k)], crecv.at[k])
        s = lax.rem(k, nbuf)
        wcopy(k).wait()
        acc[...] += lax.dot_general(wbuf[s], g[:, cols(k)], (((1,), (1,)), ((), ())),
                                    preferred_element_type=jnp.float32)

        @pl.when(k + nbuf < nk)
        def _():
            wcopy(k + nbuf).start(priority=1)

        return c

    lax.fori_loop(0, nk, step, 0)

    for d in range(1, XY):
        t = ppeer(d)[1]
        arrived(mref(t * Z, Z), mprecv.at[t])
    mc.start()
    arrived(meta.at[pl.ds((1 - core) * S, S)], mcrecv.at[0])

    info = jnp.sum(meta[...], axis=0)
    voc_dev = acc.shape[0]
    wanted = info[:1] - me * voc_dev
    logits = acc[...]
    top = jnp.max(logits, axis=0, keepdims=True)
    expsum = jnp.sum(jnp.exp(logits - top), axis=0, keepdims=True)
    entry = lax.broadcasted_iota(jnp.int32, logits.shape, 0)
    picked = jnp.sum(jnp.where(entry == wanted, logits, 0.0), axis=0, keepdims=True)
    mine[...] = jnp.concatenate([top + jnp.log(expsum), picked], axis=0)

    def qcopy(t, src_dev):
        return pltpu.make_async_remote_copy(
            mine, sbuf.at[src_dev], qsend.at[t], qrecv.at[src_dev],
            device_id=(t // V, lax.rem(t, V)), device_id_type=MESH)

    def qstart(d, c):
        qcopy(lax.rem(me + d, N), me).start()
        return c

    def qwait(d, c):
        t = lax.rem(me + d, N)
        qcopy(t, t).wait()
        return c

    lax.fori_loop(1, N, qstart, 0)
    sbuf[me] = mine[...]

    def drain(p, c):
        for d in range(1, Z):
            zcopy(p, d).wait_send()
        for d in range(1, XY):
            pcopy(p, d).wait_send()
        ccopy(p).wait_send()
        return c

    lax.fori_loop(0, nk, drain, 0)
    for copy in mz + mp + [mc]:
        copy.wait_send()
    lax.fori_loop(1, N, qwait, 0)

    allstat = sbuf[...]
    lse = allstat[:, 0, :]
    top = jnp.max(lse, axis=0, keepdims=True)
    total = top + jnp.log(jnp.sum(jnp.exp(lse - top), axis=0, keepdims=True))
    nll = total - jnp.sum(allstat[:, 1, :], axis=0, keepdims=True)
    row = lax.broadcasted_iota(jnp.int32, (NBENCH, tokens), 0)
    lanes = lax.broadcasted_iota(jnp.int32, (NBENCH, tokens), 1)
    hot = info[1:2] == row
    place = lax.broadcasted_iota(jnp.int32, (NBENCH, 128), 1)
    diagonal = place == lax.broadcasted_iota(jnp.int32, (NBENCH, 128), 0)

    def laid(column):
        return jnp.sum(jnp.where(diagonal, column, 0.0), axis=0, keepdims=True)

    own_nll = jnp.sum(jnp.where(lanes == at + row, nll, 0.0), axis=1, keepdims=True)
    nll_out[...] = laid(own_nll)[:, :td]
    total_out[...] = laid(jnp.sum(jnp.where(hot, nll, 0.0), axis=1, keepdims=True))[:, :NBENCH]
    count_out[...] = laid(jnp.sum(jnp.where(hot, 1.0, 0.0), axis=1, keepdims=True))[:, :NBENCH]


def solution(mesh):
    ndp, V = mesh.shape["dp"], mesh.shape["vocab"]
    N = ndp * V
    X = max(1, ndp // 2)
    Y = math.gcd(X, V)
    Z = V // Y

    def body(hidden, lm_head, targets, segment, pad_mask, seq_bench):
        td, depth = hidden.shape
        voc_dev = lm_head.shape[1]
        nseq = seq_bench.shape[0]
        tokens = N * td
        nk = 16
        kc = depth // nk
        wbytes = kc * (-(-voc_dev // 8) * 8) * 2
        held = tokens * depth * 2 + tokens * (-(-voc_dev // 128) * 128) * 4
        nbuf = max(2, min(nk, ((61 << 20) - held) // wbytes))
        lead_z, lead_p = 6, 2
        S = N // 2
        dims = (X, Y, Z, V, N, kc, nk, nbuf, td, lead_z, lead_p)
        vmem = pl.BlockSpec(memory_space=pltpu.VMEM)
        hbm = pl.BlockSpec(memory_space=pltpu.MemorySpace.HBM)
        dma = pltpu.SemaphoreType.DMA
        nll, total, count = pl.pallas_call(
            functools.partial(kernel, dims),
            out_shape=[jax.ShapeDtypeStruct((1, td), jnp.float32),
                       jax.ShapeDtypeStruct((1, NBENCH), jnp.float32),
                       jax.ShapeDtypeStruct((1, NBENCH), jnp.float32)],
            in_specs=[hbm] * 6,
            out_specs=[vmem] * 3,
            scratch_shapes=[
                pltpu.VMEM((tokens, depth), jnp.bfloat16),
                pltpu.VMEM((nbuf, voc_dev, kc), jnp.bfloat16),
                pltpu.VMEM((voc_dev, tokens), jnp.float32),
                pltpu.VMEM((N, 2, tokens), jnp.int32),
                pltpu.VMEM((1, td), jnp.int32),
                pltpu.VMEM((1, td), jnp.int32),
                pltpu.VMEM((1, td), jnp.int32),
                pltpu.VMEM((1, nseq), jnp.int32),
                pltpu.VMEM((2, tokens), jnp.float32),
                pltpu.VMEM((N, 2, tokens), jnp.float32),
                dma((nbuf,)), dma, dma((4,)),
                dma((nk, Z)), dma((nk, X * Y)), dma((nk,)),
                dma((nk, Z)), dma((nk, X * Y)), dma((nk,)),
                dma((Z,)), dma((X * Y,)), dma((1,)),
                dma((Z,)), dma((X * Y,)), dma((1,)),
                dma((N,)), dma((N,)),
            ],
            compiler_params=pltpu.CompilerParams(
                collective_id=0, has_side_effects=True, vmem_limit_bytes=67043328),
        )(hidden, targets.reshape(1, td), segment.reshape(1, td), pad_mask.reshape(1, td),
          seq_bench.reshape(1, nseq), lm_head.T)
        return nll.reshape(td), total.reshape(NBENCH), count.reshape(NBENCH)

    both = ("dp", "vocab")
    in_specs = (P(both, None), P(None, both), P(both), P(both), P(both), P())
    return jax.shard_map(body, mesh=mesh, in_specs=in_specs, out_specs=(P(both), P(), P()),
                         check_vma=False)
```

time: 63.1 us -> 50.4 us (0.80)
  Pallas kernels: 55.4 us -> 46.1 us
  other arithmetic: 3.73 us -> 0 us
    pallas_call x1, Pallas kernels: 55.4 us -> 46.1 us  [body(): pl.pallas_call(functools.partial(kernel, dims), out_shape=[jax.ShapeDtype...]
    unnamed x0 -> x3, local copies, waits for them, and re-layouts: none -> 3.42 us
    slice x3 -> x0, local copies, waits for them, and re-layouts: 3.01 us -> none  [the longest x2 2.8 us: body(): return (res[:tok_dev, 0], res[:, 1], res[:, 2])]
    reduce_sum x1 -> x0, other arithmetic: 0.85 us -> none  [body(): bench = jnp.sum(jnp.where(hot, seq_bench[None, :], 0), axis=1)]
    eq x3 -> x0, other arithmetic: 0.82 us -> none  [the longest x1 0.81 us: body(): segment[1:] == segment[:-1]]
    another operation x1 -> x0, other arithmetic: 0.73 us -> none  [body(): both = jnp.stack([targets, kind]).astype(jnp.float32)]
    convert_element_type x1 -> x0, other arithmetic: 0.66 us -> none  [body(): both = jnp.stack([targets, kind]).astype(jnp.float32)]
    select_n x1 -> x0, other arithmetic: 0.66 us -> none  [body(): meta = jnp.where(lane == j, both[:, j:j + 1], meta)]
where the time goes in v1:
time: 50.4 us; the launch traced here: 50.2 us
  Pallas kernels  46.1 us (91%)
  local copies, waits for them, and re-layouts  3.42 us (7%)
  between operations  0.64 us (1%)
    pallas_call x1, Pallas kernels, body(): pl.pallas_call(functools.partial(kernel, dims), out_shape=[jax.ShapeDtype...  46.1 us
    unnamed x3, local copies, waits for them, and re-layouts  3.42 us

profile of v1, /device:TPU:0, one launch (start us, length us, event | category | flops | bytes accessed | tf_op | source)
XLA Modules:
  0.0 50.2 jit_solution(15688755702177905020)
XLA Ops:
  0.6 46.1 %shard_map.85 = (f32[1,4]{1,0:T(1,128)}, f32[1,8]{1,0:T(1,128)}, f32[1,8]{1,0:T(1,128)}) custom-call(bf16[4,8192]{1,0:T(4,128)(2,1)} %hid.1, s32[1,4]{1,0:T(1,128)} %bitcast.9, s32[1,4]{1,0:T(1,128)} %bitcast.10, s32[1,4]{1,0:T(1,128)} %bitcast.11, s32[1,33]{1,0:T(1,128)} %bitcast.12, bf16[4008,8192]{1,0:T(8,128)(2,1)} %bitcast.8), custom_call_target="tpu_custom_call" | custom-call | tf_op jit(solution)/shard_map/pallas_call | solution.py:256
  46.8 1.1 %copy.12 = f32[4]{0:T(128)} copy(f32[4]{0:T(128)} %bitcast.15) | data formatting | bytes 32
  47.9 1.1 %copy.13 = f32[8]{0:T(128)} copy(f32[8]{0:T(128)} %bitcast.14) | data formatting | bytes 64
  49.0 1.2 %copy.14 = f32[8]{0:T(128)} copy(f32[8]{0:T(128)} %bitcast.13) | data formatting | bytes 64
